TPU v7x, 32 devices: a whole 2x2x4 slice. The times are simulated.
32 devices in a mesh: row: 4 (over y, x), col: 4 (over z), grp: 2 (over core).
Axes of the slice: x: 2, y: 2, z: 4, core: 2. Of those that a mesh axis runs over, the one named last changes fastest.
Arguments:
- krylov_basis: float32 [30, 8, 8192], P(None, None, 'row'), may hold values from -6 to 6
- lattice: int32 [3, 8192], P(None, 'row'), may hold values from 0 to 95, as said below
- strength_index: int32 [8192], P('row'), may hold values from 0 to 15
- strength_table: float32 [16], replicated, may hold values from 0.05 to 0.4
Outputs:
- new_block: float32 [8, 8192], P(None, 'row')
- hessenberg: float32 [30, 2, 4, 4], replicated
- block_gram: float32 [2, 4, 4], replicated
Inputs may be any that keep to these rules, and one draw needn't show every extreme that they name: The 8192 scatterers stand on distinct lattice points.
All inputs are finite; a program needn't handle non-finite values.
Results may differ from a plain program's by a relative error of at most 0.0003.
Values may be sent and summed in bfloat16 or wider, within the bound.
A program may use at most 64 MiB of HBM per device.

v0:
```python
import functools
import math

import jax
import jax.numpy as jnp
from jax import lax
from jax.experimental import pallas as pl
from jax.experimental.pallas import tpu as pltpu
from jax.sharding import PartitionSpec as P

SIN = (
    4.44286778433447,
    -7.307438665833745,
    3.5947423983311806,
    -0.784252203260472,
)
COS = (
    1.4142134959114503,
    -6.978850883575629,
    5.7394586581074964,
    -1.883544228620758,
    0.3106553287502758,
)
f32 = jnp.float32
bf16 = jnp.bfloat16
MESH = pl.DeviceIdType.MESH


def poly(u, coefs):
    value = jnp.full_like(u, coefs[-1])
    for c in coefs[-2::-1]:
        value = value * u + c
    return value


def green(squared, masked):
    inverse = lax.rsqrt(squared)
    if masked:
        inverse = jnp.where(squared > 0.5, inverse, 0.0)
    half_turns = squared * inverse * (1.0 / math.pi)
    r = half_turns - jnp.round(half_turns)
    u = r * r
    s = r * poly(u, SIN)
    scaled = s * inverse
    real_part = inverse - s * scaled
    imag_part = scaled * poly(u, COS)
    return real_part.astype(bf16), imag_part.astype(bf16)


def features(sites, is_source):
    x = sites.astype(f32)
    norm = jnp.sum(x * x, axis=0, keepdims=True)
    high = jnp.floor(norm * (1.0 / 256.0)) * 256.0
    low = norm - high
    one = jnp.ones_like(norm)
    if is_source:
        parts = [-2.0 * x, one, one, high, low, jnp.zeros_like(norm)]
    else:
        parts = [x, high, low, one, one, jnp.zeros_like(norm)]
    return jnp.concatenate(parts, 0)


def split(x):
    high = x.astype(bf16)
    return high, (x - high.astype(f32)).astype(bf16)


def turn_rows(x):
    half = x.shape[0] // 2
    return jnp.concatenate([x[half:], -x[:half]], 0)


def turn_lanes(x, ch):
    half = ch // 2
    lane = lax.broadcasted_iota(jnp.int32, x.shape, 1)
    return jnp.where(
        lane % ch < half, pltpu.roll(x, x.shape[1] - half, 1), -pltpu.roll(x, half, 1)
    )


def lift(x):
    return x + turn_lanes(turn_rows(x), x.shape[0])


def dot(x, y, numbers=(((1,), (0,)), ((), ()))):
    return lax.dot_general(
        x, y, numbers, precision=lax.Precision.HIGHEST, preferred_element_type=f32
    )


lanes = (((1,), (1,)), ((), ()))


def kernel(
    dims, table_hbm, basis_hbm, lattice_hbm, index_hbm, coef_ref, gram_ref, new_ref,
    table_ref, direction, lattice_ref, index_ref,
    basis, high, low, overlap, halves, metric, gath, tgt, partial, landed, field, coef,
    copy_sem, send1, recv1, send2, recv2, send3, recv3, send4, recv4, send5, recv5,
):
    R, C, G, blk, points, nb, ch, table = dims
    parts = C * G
    T = parts * blk
    K = nb * ch
    KP = basis.shape[0]
    half = ch // 2
    blocks = KP // ch
    planes = KP // 128
    row, col, grp = lax.axis_index("row"), lax.axis_index("col"), lax.axis_index("grp")
    me = col * G + grp
    own = pl.ds(pl.multiple_of(me * blk, blk), blk)
    loads = [
        pltpu.make_async_copy(lattice_hbm, lattice_ref, copy_sem.at[0]),
        pltpu.make_async_copy(index_hbm.at[:, own], index_ref, copy_sem.at[1]),
        pltpu.make_async_copy(basis_hbm.at[pl.ds(K - ch, ch), own], direction, copy_sem.at[2]),
        pltpu.make_async_copy(table_hbm, table_ref, copy_sem.at[3]),
        pltpu.make_async_copy(basis_hbm, basis.at[pl.ds(0, K)], copy_sem.at[4]),
    ]
    for load in loads:
        load.start()

    barrier = pltpu.get_barrier_semaphore()
    for k in range(1, R):
        pl.semaphore_signal(
            barrier, inc=1, device_id={"row": lax.rem(row + k, R)}, device_id_type=MESH
        )
    for k in range(1, parts):
        other = lax.rem(me + k, parts)
        pl.semaphore_signal(
            barrier, inc=1, device_id={"col": other // G, "grp": lax.rem(other, G)},
            device_id_type=MESH,
        )

    if KP > K:
        basis[K:] = jnp.zeros((KP - K, T), f32)
    overlap[...] = jnp.zeros_like(overlap)
    for load in loads[:4]:
        load.wait()
    index = index_ref[...]
    strength = jnp.zeros(index.shape, f32)
    for entry in range(table):
        strength = jnp.where(index == entry, table_ref[entry], strength)
    sources = features(lattice_ref[:, own], True)
    gath[pl.ds(row, 1)] = jnp.concatenate([direction[...] * strength, sources], 0).astype(bf16)[
        None
    ]
    zeros = jnp.zeros((8, T), f32)
    tgt[...] = jnp.concatenate([features(lattice_ref[...], False), zeros], 0).astype(bf16)

    def row_copy(ref, sends, recvs, slot, peer):
        return pltpu.make_async_remote_copy(
            src_ref=ref.at[slot], dst_ref=ref.at[slot], send_sem=sends.at[peer],
            recv_sem=recvs.at[slot], device_id={"row": peer}, device_id_type=MESH,
        )

    def row_send(ref, sends, recvs):
        for k in range(1, R):
            row_copy(ref, sends, recvs, row, lax.rem(row + k, R)).start()

    def row_wait(ref, sends, recvs):
        for k in range(1, R):
            peer = lax.rem(row + k, R)
            copy = row_copy(ref, sends, recvs, peer, peer)
            copy.wait_recv()
            copy.wait_send()

    def scatter(chunk, part, masked=False):
        block = gath[pl.ds(chunk, 1)][0].astype(f32)
        weights = block[:8]
        direct = weights.astype(bf16)
        turned = jnp.concatenate([-weights[4:], weights[:4]], 0).astype(bf16)
        sites = jnp.concatenate([block[8:], jnp.zeros((8, blk), f32)], 0).T.astype(bf16)
        at = pl.ds(pl.multiple_of(part * blk, blk), blk)
        targets = tgt[:, at]
        squared = jnp.dot(sites, targets, preferred_element_type=f32)
        real_part, imag_part = green(squared, masked)
        return jnp.dot(direct, real_part, preferred_element_type=f32) + jnp.dot(
            turned, imag_part, preferred_element_type=f32
        )

    def target_of(left):
        left_col = lax.div(left, G)
        if C & (C - 1):
            to_col = lax.rem(col + left_col, C)
        else:
            to_col = 0
            for bit in range(C.bit_length() - 1):
                size = 1 << bit
                to_col = to_col + lax.rem(lax.div(col, size) + lax.div(left_col, size), 2) * size
        to_grp = lax.rem(grp + left, G)
        return to_col, to_grp

    def basis_slice(part):
        at = pl.ds(pl.multiple_of(part * blk, blk), blk)
        b_high, b_low = split(basis[:, at])
        high[:, at] = b_high
        low[:, at] = b_low
        return b_high, b_low

    def store_first(part, masked):
        partial[pl.ds(part, 1)] = scatter(row, part, masked)[None]

    store_first(me, True)
    early = max(parts // 2, 1)

    @pl.loop(1, early)
    def _(left):
        to_col, to_grp = target_of(left)
        store_first(to_col * G + to_grp, False)

    pl.semaphore_wait(barrier, R - 1 + parts - 1)
    row_send(gath, send1, recv1)
    loads[4].wait()
    late = parts - early
    each = parts // late

    @pl.loop(early, parts)
    def _(left):
        to_col, to_grp = target_of(left)
        store_first(to_col * G + to_grp, False)
        left_part, right_part = [], []
        for i in range(each):
            b_high, b_low = basis_slice((left - early) * each + i)
            left_part += [b_high, b_high]
            right_part += [b_high * bf16(0.5), b_low]
        products = lax.dot_general(
            jnp.concatenate(left_part, 1), jnp.concatenate(right_part, 1), lanes,
            preferred_element_type=f32,
        )
        for p in range(planes):
            overlap[p] += products[:, p * 128:(p + 1) * 128]

    summed = jnp.concatenate([overlap[p] for p in range(planes)], 1)
    summed = summed + summed.T
    for p in range(planes):
        overlap[p] = summed[:, p * 128:(p + 1) * 128]
    for a in range(half):
        for p in range(planes):
            upper = overlap[p, pl.ds(a, blocks, stride=ch), :]
            lower = overlap[p, pl.ds(a + half, blocks, stride=ch), :]
            halves[pl.ds(row, 1), pl.ds(a * blocks, blocks), p * 128:(p + 1) * 128] = (
                upper + turn_lanes(lower, ch)
            )[None]
    row_wait(gath, send1, recv1)
    row_send(halves, send5, recv5)

    def part_send(part, to_col, to_grp):
        return pltpu.make_async_remote_copy(
            src_ref=partial.at[part], dst_ref=landed.at[me], send_sem=send2.at[part],
            recv_sem=recv2.at[me], device_id={"col": to_col, "grp": to_grp}, device_id_type=MESH,
        )

    @pl.loop(0, parts)
    def _(k):
        to_col, to_grp = target_of(parts - 1 - k)
        part = to_col * G + to_grp

        def more(q, total):
            return total + scatter(lax.rem(row + q, R), part)

        total = lax.fori_loop(1, R, more, partial[pl.ds(part, 1)][0], unroll=R <= 4)
        partial[pl.ds(part, 1)] = total[None]

        @pl.when(k < parts - 1)
        def _():
            part_send(part, to_col, to_grp).start()

    total = partial[pl.ds(me, 1)][0]
    for k in range(1, parts):
        other = lax.rem(me + k, parts)
        copy = pltpu.make_async_remote_copy(
            src_ref=partial.at[other], dst_ref=landed.at[other], send_sem=send2.at[other],
            recv_sem=recv2.at[other], device_id={"col": other // G, "grp": lax.rem(other, G)},
            device_id_type=MESH,
        )
        copy.wait_recv()
        copy.wait_send()
        total = total + landed[pl.ds(other, 1)][0]
    field[:, own] = total

    def field_copy(slot, to):
        at = pl.ds(pl.multiple_of(slot * blk, blk), blk)
        return pltpu.make_async_remote_copy(
            src_ref=field.at[:, at], dst_ref=field.at[:, at], send_sem=send3.at[to],
            recv_sem=recv3.at[slot], device_id={"col": to // G, "grp": lax.rem(to, G)},
            device_id_type=MESH,
        )

    def peer_of(left):
        to_col, to_grp = target_of(jnp.int32(left))
        return to_col * G + to_grp

    for left in range(parts - 1, 0, -1):
        field_copy(me, peer_of(left)).start()

    def stack(x):
        x_high, x_low = split(x)
        return jnp.concatenate([x_high.astype(f32), x_low.astype(f32)], 0).astype(bf16)

    def piece(part):
        at = pl.ds(pl.multiple_of(part * blk, blk), blk)
        stacked = stack(field[:, at])
        out = lax.dot_general(
            jnp.concatenate([stacked, stacked], 1),
            jnp.concatenate([high[:, at], low[:, at]], 1),
            lanes, preferred_element_type=f32,
        )
        norm = lax.dot_general(stacked, stacked, lanes, preferred_element_type=f32)
        return out, norm

    out, norm = piece(me)
    for left in range(1, parts):
        other = peer_of(left)
        copy = field_copy(other, other)
        copy.wait_recv()
        copy.wait_send()
        more_out, more_norm = piece(other)
        out, norm = out + more_out, norm + more_norm
    coef[pl.ds(row, 1), :, :KP] = (out[:ch] + out[ch:])[None]
    coef[pl.ds(row, 1), :, KP:] = jnp.zeros((1, ch, 128), f32)
    norm = norm[:ch] + norm[ch:]
    coef[pl.ds(row, 1), :, pl.ds(KP, ch)] = (norm[:, :ch] + norm[:, ch:])[None]
    row_send(coef, send4, recv4)

    scale = 1.0 / points
    row_wait(halves, send5, recv5)
    for a in range(half):
        rows = jnp.sum(halves[:, pl.ds(a * blocks, blocks), :], 0) * scale
        turned = -turn_lanes(rows, ch)
        for p in range(planes):
            at = slice(p * 128, (p + 1) * 128)
            metric[p, pl.ds(a, blocks, stride=ch), :] = rows[:, at]
            metric[p, pl.ds(a + half, blocks, stride=ch), :] = turned[:, at]
    full = jnp.concatenate([metric[p] for p in range(planes)], 1)
    full_high, full_low = split(full)

    def apply(x, x_high, x_low):
        stacked = stack(x)
        out = jnp.dot(stacked, x_high, preferred_element_type=f32)
        out = out + jnp.dot(stacked, x_low, preferred_element_type=f32)
        return out[:ch] + out[ch:]

    row_wait(coef, send4, recv4)
    sums = jnp.sum(coef[...], 0) * scale
    mixed = lift(sums[:, :KP])
    self_gram = lift(sums[:, KP:])[:, :ch]
    once = full[K - ch:K] - mixed
    twice = once - apply(once, full_high, full_low)
    both = once + twice
    coef_ref[...] = both
    at_row = lax.broadcasted_iota(jnp.int32, both.shape, 0)
    at_lane = lax.broadcasted_iota(jnp.int32, both.shape, 1)
    change = both - jnp.where(at_lane == at_row + (K - ch), 1.0, 0.0)
    new_ref[...] = -(field[...] + apply(change, high[...], low[...]))
    cross = dot(mixed, change, lanes)
    cross_t = dot(change, mixed, lanes)
    gram_ref[...] = jnp.zeros_like(gram_ref)
    gram_ref[:, :ch] = self_gram + cross + cross_t + dot(
        apply(change, full_high, full_low), change, lanes
    )


def local(krylov_basis, lattice, strength_index, strength_table):
    R, C, G = (lax.axis_size(a) for a in ("row", "col", "grp"))
    nb, ch, T = krylov_basis.shape
    parts = C * G
    blk = T // parts
    K = nb * ch
    KP = -(-K // 128) * 128
    table = strength_table.shape[0]
    dims = (R, C, G, blk, T * R, nb, ch, table)
    vmem = pl.BlockSpec(memory_space=pltpu.VMEM)
    hbm = pl.BlockSpec(memory_space=pltpu.HBM)
    dma = pltpu.SemaphoreType.DMA
    coefs, gram, new_block = pl.pallas_call(
        functools.partial(kernel, dims),
        out_shape=(
            jax.ShapeDtypeStruct((ch, KP), f32),
            jax.ShapeDtypeStruct((ch, 128), f32),
            jax.ShapeDtypeStruct((ch, T), f32),
        ),
        in_specs=[hbm, hbm, hbm, hbm],
        out_specs=(vmem, vmem, vmem),
        scratch_shapes=[
            pltpu.SMEM((table,), f32),
            pltpu.VMEM((ch, blk), f32),
            pltpu.VMEM((3, T), jnp.int32),
            pltpu.VMEM((1, blk), jnp.int32),
            pltpu.VMEM((KP, T), f32),
            pltpu.VMEM((KP, T), bf16),
            pltpu.VMEM((KP, T), bf16),
            pltpu.VMEM((KP // 128, KP, 128), f32),
            pltpu.VMEM((R, KP // 2, KP), f32),
            pltpu.VMEM((KP // 128, KP, 128), f32),
            pltpu.VMEM((R, 16, blk), bf16),
            pltpu.VMEM((16, T), bf16),
            pltpu.VMEM((parts, ch, blk), f32),
            pltpu.VMEM((parts, ch, blk), f32),
            pltpu.VMEM((ch, T), f32),
            pltpu.VMEM((R, ch, KP + 128), f32),
            dma((5,)),
            dma((R,)), dma((R,)),
            dma((parts,)), dma((parts,)),
            dma((parts,)), dma((parts,)),
            dma((R,)), dma((R,)),
            dma((R,)), dma((R,)),
        ],
        compiler_params=pltpu.CompilerParams(
            collective_id=0, has_side_effects=True, vmem_limit_bytes=50331648
        ),
        name="foldy_step",
    )(*[pltpu.with_memory_space_constraint(v, pltpu.HBM) for v in (strength_table, krylov_basis.reshape(K, T), lattice, strength_index.reshape(1, T))])
    half = ch // 2
    mixing = coefs[:, :K].reshape(2, half, nb, ch)[..., :half]
    hessenberg = mixing.transpose(2, 0, 3, 1)
    block_gram = jnp.stack([gram[:half, :half], gram[:half, half:ch]], 0)
    return (new_block, hessenberg, block_gram)


def solution(mesh):
    in_specs = (P(None, None, "row"), P(None, "row"), P("row"), P())
    out_specs = (P(None, "row"), P(), P())
    return jax.shard_map(local, mesh=mesh, in_specs=in_specs, out_specs=out_specs, check_vma=False)
```

profile of v0, /device:TPU:0, one launch (start us, length us, event | category | flops | bytes accessed | tf_op | source)
XLA Modules:
  0.0 31.2 jit_solution(9904457637429938225)
XLA Ops:
  0.6 28.4 %foldy_step.1 = (f32[8,256]{1,0:T(8,128)S(1)}, f32[8,128]{1,0:T(8,128)S(1)}, f32[8,2048]{1,0:T(8,128)S(1)}) custom-call(f32[16]{0:T(128)} %table_hbm.1, f32[240,2048]{1,0:T(8,128)} %bitcast.10, s32[3,2048]{1,0:T(4,128)} %lattice_hbm.1, s32[1,2048]{1,0:T(1,128)} %bitcast.11), custom_call_target="tpu_custom_call" | custom-call | tf_op jit(solution)/shard_map/foldy_step/pallas_call | solution.py:374
  29.0 0.1 slice_bitcast_fusion.2
  29.1 0.6 %pad_maximum_fusion = f32[2,4,4]{2,1,0:T(4,128)} fusion(f32[1,4,4]{2,1,0:T(4,128)S(1)} %get-tuple-element.13, f32[1,4,4]{2,1,0:T(4,128)S(1)} %get-tuple-element.12), kind=kLoop, calls=%fused_computation.1 | loop fusion | flops 32 | bytes 256 | tf_op jit(solution)/shard_map/stack | solution.py:415
  29.7 0.1 reshape.17
  29.8 0.7 %copy.8 = f32[30,2,4,4]{0,3,2,1:T(4,128)} copy(f32[30,2,4,4]{2,0,3,1:T(8,128)S(1)} %slice_bitcast_fusion) | data formatting | bytes 7680
  30.6 0.6 %copy.10 = f32[8,2048]{1,0:T(8,128)} copy(f32[8,2048]{1,0:T(8,128)S(1)} %get-tuple-element.17) | data formatting | bytes 131072
  (1 shorter events, 0.0 us)
where the time goes:
time: 31.3 us; the launch traced here: 31.2 us
  Pallas kernels  28.4 us (91%)
  local copies, waits for them, and re-layouts  1.54 us (5%)
  between operations  0.66 us (2%)
  other arithmetic  0.6 us (2%)
    pallas_call x1, Pallas kernels, local(): pl.pallas_call(functools.partial(kernel, dims), out_shape=(jax.ShapeDtype...  28.4 us
    unnamed x2, local copies, waits for them, and re-layouts  1.36 us

commit v1 on v0

v1 whole, which is shorter than its diff:
```python
import functools
import math

import jax
import jax.numpy as jnp
from jax import lax
from jax.experimental import pallas as pl
from jax.experimental.pallas import tpu as pltpu
from jax.sharding import PartitionSpec as P

SIN = (4.4428408013470655, -7.306699927693229, 3.5893875730482314, -0.7728270191086756)
f32 = jnp.float32
bf16 = jnp.bfloat16
MESH = pl.DeviceIdType.MESH


def poly(u, coefs):
    value = jnp.full_like(u, coefs[-1])
    for c in coefs[-2::-1]:
        value = value * u + c
    return value


def green(squared, masked):
    inverse = lax.rsqrt(squared)
    if masked:
        inverse = jnp.where(squared > 0.5, inverse, 0.0)
    half_turns = squared * inverse * (1.0 / math.pi)
    r = half_turns - jnp.round(half_turns)
    s = r * poly(r * r, SIN)
    twice = s * s
    rest = jnp.maximum(2.0 - twice, 1e-12)
    c = rest * lax.rsqrt(rest)
    real_part = inverse - twice * inverse
    imag_part = s * inverse * c
    return real_part.astype(bf16), imag_part.astype(bf16)


def features(sites, is_source):
    x = sites.astype(f32)
    norm = jnp.sum(x * x, axis=0, keepdims=True)
    high = jnp.floor(norm * (1.0 / 256.0)) * 256.0
    low = norm - high
    one = jnp.ones_like(norm)
    if is_source:
        parts = [-2.0 * x, one, one, high, low, jnp.zeros_like(norm)]
    else:
        parts = [x, high, low, one, one, jnp.zeros_like(norm)]
    return jnp.concatenate(parts, 0)


def split(x):
    high = x.astype(bf16)
    return high, (x - high.astype(f32)).astype(bf16)


def stack(x):
    x_high, x_low = split(x)
    return jnp.concatenate([x_high.astype(f32), x_low.astype(f32)], 0).astype(bf16)


def times_i(x):
    half = x.shape[0] // 2
    return jnp.concatenate([-x[half:], x[:half]], 0)


def fold(x):
    half = x.shape[0] // 2
    return x[:half] + x[half:]


lanes = (((1,), (1,)), ((), ()))


def bit_of(x, size):
    return (x // size) % 2 if isinstance(x, int) else lax.rem(lax.div(x, size), 2)


def xor(a, b, n):
    out = 0
    size = 1
    while size < n:
        out = out + lax.rem(bit_of(a, size) + bit_of(b, size), 2) * size
        size *= 2
    return out


def kernel(
    dims, table_hbm, basis_hbm, lattice_hbm, index_hbm, hess_ref, gram_ref, new_ref,
    table_ref, direction, lattice_ref, index_ref, basis, high, low, tgt, gath,
    overlap, metric, partial, landed, field, near, far,
    copy_sem, *sems,
):
    R, C, G, blk, points, nb, NB, ch, table = dims
    parts = C * G
    T = parts * blk
    K = nb * ch
    half = ch // 2
    KP = NB * ch
    HK = NB * half
    (send_g, recv_g, send_h, recv_h, send_p, recv_p, send_f, recv_f, send_n, recv_n,
     send_z, recv_z) = sems
    row, col, grp = lax.axis_index("row"), lax.axis_index("col"), lax.axis_index("grp")
    me = col * G + grp

    def at(part):
        return pl.ds(pl.multiple_of(part * blk, blk), blk)

    own = at(me)
    loads = [
        pltpu.make_async_copy(lattice_hbm, lattice_ref, copy_sem.at[0]),
        pltpu.make_async_copy(index_hbm.at[:, own], index_ref, copy_sem.at[1]),
        pltpu.make_async_copy(basis_hbm.at[pl.ds(K - ch, ch), own], direction, copy_sem.at[2]),
        pltpu.make_async_copy(table_hbm, table_ref, copy_sem.at[3]),
    ]
    for v in range(T // 128):
        loads.append(pltpu.make_async_copy(
            basis_hbm.at[:, pl.ds(v * 128, 128)], basis.at[v, pl.ds(0, K)], copy_sem.at[4 + v]
        ))
    for load in loads:
        load.start()

    def row_id(other):
        return {"row": other}

    def part_id(other):
        return {"col": lax.div(other, G), "grp": lax.rem(other, G)}

    row_peer = [row] + [xor(row, q, R) for q in range(1, R)]
    part_peer = [me] + [xor(me, s, parts) for s in range(1, parts)]
    barrier = pltpu.get_barrier_semaphore()
    for q in range(1, R):
        pl.semaphore_signal(barrier, inc=1, device_id=row_id(row_peer[q]), device_id_type=MESH)
    for s in range(1, parts):
        pl.semaphore_signal(barrier, inc=1, device_id=part_id(part_peer[s]), device_id_type=MESH)

    def copy_to(src, dst, send, recv, device):
        return pltpu.make_async_remote_copy(
            src_ref=src, dst_ref=dst, send_sem=send, recv_sem=recv, device_id=device,
            device_id_type=MESH,
        )

    basis[:, K:] = jnp.zeros((T // 128, KP - K, 128), f32)
    for load in loads[:4]:
        load.wait()
    index = index_ref[...]
    strength = jnp.zeros(index.shape, f32)
    for entry in range(table):
        strength = jnp.where(index == entry, table_ref[entry], strength)
    own_sites = features(lattice_ref[:, own], True)
    gath[0] = jnp.concatenate([direction[...] * strength, own_sites], 0).astype(bf16)
    zeros = jnp.zeros((8, T), f32)
    tgt[...] = jnp.concatenate([features(lattice_ref[...], False), zeros], 0).astype(bf16)

    def source(slot):
        block = gath[slot].astype(f32)
        sent = block[:ch]
        both = jnp.concatenate([sent, times_i(sent)], 1).astype(bf16)
        sites = jnp.concatenate([block[ch:], jnp.zeros((8, blk), f32)], 0).T.astype(bf16)
        return sites, both

    def pair(src, part, masked=False):
        sites, both = src
        squared = jnp.dot(sites, tgt[:, at(part)], preferred_element_type=f32)
        real_part, imag_part = green(squared, masked)
        return jnp.dot(both, jnp.concatenate([real_part, imag_part], 0), preferred_element_type=f32)

    mine = source(0)
    partial[pl.ds(me, 1)] = pair(mine, me, True)[None]
    for s in range(1, parts):
        partial[pl.ds(part_peer[s], 1)] = pair(mine, part_peer[s])[None]

    pl.semaphore_wait(barrier, R - 1 + parts - 1)
    gathers = [
        copy_to(gath.at[0], gath.at[q], send_g.at[q], recv_g.at[q], row_id(row_peer[q]))
        if q else None for q in range(R)
    ]
    for q in range(R - 1, 0, -1):
        gathers[q].start()

    for load in loads[4:]:
        load.wait()
    overlap[...] = jnp.zeros_like(overlap)
    each = 2

    @pl.loop(0, parts // each)
    def _(i):
        left, right = [], []
        for k in range(each):
            span = at(i * each + k)
            rows = jnp.concatenate(
                [
                    jnp.concatenate(
                        [basis[(i * each + k) * (blk // 128) + v, pl.ds(c, NB, stride=ch), :]
                         for v in range(blk // 128)], 1,
                    )
                    for c in range(ch)
                ], 0,
            )
            b_high, b_low = split(rows)
            high[:, span] = b_high
            low[:, span] = b_low
            left += [b_high, b_high]
            right += [b_high * bf16(0.5), b_low]
        products = lax.dot_general(
            jnp.concatenate(left, 1), jnp.concatenate(right, 1), lanes, preferred_element_type=f32
        )
        overlap[0] += products[:HK, :HK] + products[HK:, HK:]
        overlap[1] += products[:HK, HK:] - products[HK:, :HK]

    even, odd = overlap[0], overlap[1]
    metric[pl.ds(row, 1)] = jnp.concatenate([even + even.T, odd - odd.T], 1)[None]
    for q in range(1, R):
        copy_to(metric.at[row], metric.at[row], send_h.at[q], recv_h.at[row], row_id(row_peer[q])).start()

    for q in range(1, R):
        gathers[q].wait()

    def part_copy(s):
        return copy_to(
            partial.at[part_peer[s]], landed.at[s], send_p.at[s], recv_p.at[s], part_id(part_peer[s])
        )

    def off_row(part, sources):
        total = partial[pl.ds(part, 1)][0]
        for src in sources:
            total = total + pair(src, part)
        return total

    if (R - 1) * parts <= 32:
        sources = [source(q) for q in range(1, R)]
        for s in range(parts - 1, 0, -1):
            partial[pl.ds(part_peer[s], 1)] = off_row(part_peer[s], sources)[None]
            part_copy(s).start()
        total = off_row(me, sources)
    else:
        @pl.loop(0, parts - 1)
        def _(k):
            s = parts - 1 - k
            part = xor(me, s, parts)
            partial[pl.ds(part, 1)] = off_row(part, [source(q) for q in range(1, R)])[None]
            copy_to(partial.at[part], landed.at[s], send_p.at[s], recv_p.at[s], part_id(part)).start()

        total = off_row(me, [source(q) for q in range(1, R)])
    for s in range(parts - 1, 0, -1):
        part_copy(s).wait()
        total = total + landed[s]
    field[:, own] = total

    def field_copy(s, part):
        return copy_to(
            field.at[:, at(part)], field.at[:, at(part)], send_f.at[s], recv_f.at[s],
            part_id(part_peer[s]),
        )


    scale = 1.0 / points
    stacked = stack(total)
    raw = fold(lax.dot_general(
        jnp.concatenate([stacked, stacked], 1), jnp.concatenate([high[:, own], low[:, own]], 1),
        lanes, preferred_element_type=f32,
    ))
    norm = fold(lax.dot_general(stacked, stacked, lanes, preferred_element_type=f32))
    norm = norm[:, :ch] + norm[:, ch:]
    coef = raw[:, :HK] - times_i(raw[:, HK:])
    norm = norm[:, :half] - times_i(norm[:, half:])
    lane = lax.broadcasted_iota(jnp.int32, (ch, HK), 1)
    for a in range(half):
        coef = jnp.where(lane == a * NB + nb, norm[:, a:a + 1], coef)
    near[pl.ds(row, 1)] = coef[None]
    for q in range(R - 1, 0, -1):
        copy_to(near.at[row], near.at[row], send_n.at[q], recv_n.at[row], row_id(row_peer[q])).start()
    for s in range(parts - 1, 0, -1):
        field_copy(s, me).start()

    for q in range(1, R):
        peer = row_peer[q]
        copy_to(metric.at[peer], metric.at[peer], send_h.at[q], recv_h.at[peer], row_id(peer)).wait()
    full = jnp.sum(metric[...], 0) * scale
    full_high, full_low = split(full)
    full_both = jnp.concatenate([full_high, full_low], 0)
    overlap[0], overlap[1] = full[:, :HK], full[:, HK:]
    last = pl.ds(nb - 1, half, stride=NB)
    once = jnp.concatenate([overlap[0, last, :], -overlap[1, last, :]], 0)

    for q in range(1, R):
        peer = row_peer[q]
        copy_to(near.at[peer], near.at[peer], send_n.at[q], recv_n.at[peer], row_id(peer)).wait()
    far[pl.ds(me, 1)] = jnp.sum(near[...], 0)[None]
    for s in range(parts - 1, 0, -1):
        copy_to(far.at[me], far.at[me], send_z.at[s], recv_z.at[me], part_id(part_peer[s])).start()
    for s in range(1, parts):
        field_copy(s, part_peer[s]).wait()
    for s in range(1, parts):
        peer = part_peer[s]
        copy_to(far.at[peer], far.at[peer], send_z.at[s], recv_z.at[peer], part_id(peer)).wait()
    sums = jnp.sum(far[...], 0) * scale

    def apply(x):
        x16 = stack(x)
        y = fold(jnp.dot(jnp.concatenate([x16, x16], 1), full_both, preferred_element_type=f32))
        return y[:, :HK] - times_i(y[:, HK:])

    in_basis = lax.rem(lane, NB) < nb
    at_row = lax.broadcasted_iota(jnp.int32, (ch, HK), 0)
    mixed = jnp.where(in_basis, sums, 0.0)
    once = once - mixed
    both = 2.0 * once - apply(once)
    change = both - jnp.where(lane == at_row * NB + (nb - 1), 1.0, 0.0)
    lifted = stack(jnp.concatenate([change, times_i(change)], 1))
    for part in range(parts):
        cols = slice(part * blk, (part + 1) * blk)
        out = jnp.dot(lifted, high[:, cols], preferred_element_type=f32)
        out = out + jnp.dot(lifted, low[:, cols], preferred_element_type=f32)
        new_ref[:, cols] = -(field[:, cols] + fold(out))
    for i in range(2):
        for a in range(half):
            hess_ref[i, a] = both[i * half:(i + 1) * half, a * NB:a * NB + nb]
    other = mixed + apply(change)
    cross = fold(lax.dot_general(
        stack(jnp.concatenate([change, mixed], 1)), stack(jnp.concatenate([other, change], 1)),
        lanes, preferred_element_type=f32,
    ))
    cross = cross[:, :ch] + cross[:, ch:]
    self_gram = jnp.concatenate([sums[:, a * NB + nb:a * NB + nb + 1] for a in range(half)], 1)
    gram_ref[0] = self_gram[:half].T + cross[:half, :half] + cross[half:, half:]
    gram_ref[1] = self_gram[half:].T + cross[:half, half:] - cross[half:, :half]


def local(krylov_basis, lattice, strength_index, strength_table):
    R, C, G = (lax.axis_size(a) for a in ("row", "col", "grp"))
    nb, ch, T = krylov_basis.shape
    parts = C * G
    blk = T // parts
    K = nb * ch
    half = ch // 2
    NB = -(-(nb + 1) // 32) * 32
    KP, HK = NB * ch, NB * half
    table = strength_table.shape[0]
    dims = (R, C, G, blk, T * R, nb, NB, ch, table)
    vmem = pl.BlockSpec(memory_space=pltpu.VMEM)
    hbm = pl.BlockSpec(memory_space=pltpu.HBM)
    dma = pltpu.SemaphoreType.DMA
    hess, gram, new_block = pl.pallas_call(
        functools.partial(kernel, dims),
        out_shape=(
            jax.ShapeDtypeStruct((2, half, half, nb), f32),
            jax.ShapeDtypeStruct((2, half, half), f32),
            jax.ShapeDtypeStruct((ch, T), f32),
        ),
        in_specs=[hbm, hbm, hbm, hbm],
        out_specs=(vmem, vmem, vmem),
        scratch_shapes=[
            pltpu.SMEM((table,), f32),
            pltpu.VMEM((ch, blk), f32),
            pltpu.VMEM((3, T), jnp.int32),
            pltpu.VMEM((1, blk), jnp.int32),
            pltpu.VMEM((T // 128, KP, 128), f32),
            pltpu.VMEM((KP, T), bf16),
            pltpu.VMEM((KP, T), bf16),
            pltpu.VMEM((16, T), bf16),
            pltpu.VMEM((R, 16, blk), bf16),
            pltpu.VMEM((2, HK, HK), f32),
            pltpu.VMEM((R, HK, 2 * HK), f32),
            pltpu.VMEM((parts, ch, blk), f32),
            pltpu.VMEM((parts, ch, blk), f32),
            pltpu.VMEM((ch, T), f32),
            pltpu.VMEM((R, ch, HK), f32),
            pltpu.VMEM((parts, ch, HK), f32),
            dma((4 + T // 128,)),
            dma((R,)), dma((R,)),
            dma((R,)), dma((R,)),
            dma((parts,)), dma((parts,)),
            dma((parts,)), dma((parts,)),
            dma((R,)), dma((R,)),
            dma((parts,)), dma((parts,)),
        ],
        compiler_params=pltpu.CompilerParams(
            collective_id=0, has_side_effects=True, vmem_limit_bytes=50331648
        ),
        name="foldy_step",
    )(*[pltpu.with_memory_space_constraint(v, pltpu.HBM) for v in (strength_table, krylov_basis.reshape(K, T), lattice, strength_index.reshape(1, T))])
    return (new_block, hess.transpose(3, 0, 1, 2), gram)


def solution(mesh):
    in_specs = (P(None, None, "row"), P(None, "row"), P("row"), P())
    out_specs = (P(None, "row"), P(), P())
    return jax.shard_map(local, mesh=mesh, in_specs=in_specs, out_specs=out_specs, check_vma=False)
```

time: 31.3 us -> 27.9 us (0.89)
  Pallas kernels: 28.4 us -> 25.3 us
  other arithmetic: 0.6 us -> 0 us
    pallas_call x1, Pallas kernels: 28.4 us -> 25.3 us  [local(): pl.pallas_call(functools.partial(kernel, dims), out_shape=(jax.ShapeDtype...]
    another operation x1 -> x0, other arithmetic: 0.6 us -> none  [local(): block_gram = jnp.stack([gram[:half, :half], gram[:half, half:ch]], 0)]
    unnamed x2 -> x3, local copies, waits for them, and re-layouts: 1.36 us -> 1.83 us
where the time goes in v1:
time: 27.9 us; the launch traced here: 27.7 us
  Pallas kernels  25.3 us (91%)
  local copies, waits for them, and re-layouts  1.83 us (7%)
  between operations  0.64 us (2%)
    pallas_call x1, Pallas kernels, local(): pl.pallas_call(functools.partial(kernel, dims), out_shape=(jax.ShapeDtype...  25.3 us
    unnamed x3, local copies, waits for them, and re-layouts  1.83 us

profile of v1, /device:TPU:0, one launch (start us, length us, event | category | flops | bytes accessed | tf_op | source)
XLA Modules:
  0.0 27.7 jit_solution(13084491052385069088)
XLA Ops:
  0.6 25.3 %foldy_step.1 = (f32[2,4,4,30]{3,2,1,0:T(4,128)S(1)}, f32[2,4,4]{2,1,0:T(4,128)S(1)}, f32[8,2048]{1,0:T(8,128)S(1)}) custom-call(f32[16]{0:T(128)} %table_hbm.1, f32[240,2048]{1,0:T(8,128)} %bitcast.4, s32[3,2048]{1,0:T(4,128)} %lattice_hbm.1, s32[1,2048]{1,0:T(1,128)} %bitcast.5), custom_call_target="tpu_custom_call" | custom-call | tf_op jit(solution)/shard_map/foldy_step/pallas_call | solution.py:344
  25.9 0.6 %copy.10 = f32[8,2048]{1,0:T(8,128)} copy(f32[8,2048]{1,0:T(8,128)S(1)} %get-tuple-element.12) | data formatting | bytes 131072
  26.5 0.6 %copy.11 = f32[30,2,4,4]{0,3,2,1:T(4,128)} copy(f32[30,2,4,4]{0,3,2,1:T(4,128)S(1)} %bitcast.3) | data formatting | bytes 7680
  27.1 0.6 %copy.12 = f32[2,4,4]{2,1,0:T(4,128)} copy(f32[2,4,4]{2,1,0:T(4,128)S(1)} %get-tuple-element.14) | data formatting | bytes 256

commit v2 on v1

v2 whole, which is shorter than its diff:
```python
import functools
import math

import jax
import jax.numpy as jnp
from jax import lax
from jax.experimental import pallas as pl
from jax.experimental.pallas import tpu as pltpu
from jax.sharding import PartitionSpec as P

SIN = (4.442834924970635, -7.306550394807036, 3.5883736565798134, -0.7707881588297861)
f32 = jnp.float32
bf16 = jnp.bfloat16
MESH = pl.DeviceIdType.MESH


def poly(u, coefs):
    value = jnp.full_like(u, coefs[-1])
    for c in coefs[-2::-1]:
        value = value * u + c
    return value


def green(squared, masked):
    inverse = lax.rsqrt(squared)
    if masked:
        inverse = jnp.where(squared > 0.5, inverse, 0.0)
    half_turns = squared * inverse * (1.0 / math.pi)
    r = half_turns - jnp.round(half_turns)
    s = r * poly(r * r, SIN)
    rest = jnp.maximum(2.0 - s * s, 1e-12)
    scaled = rest * inverse
    real_part = scaled - inverse
    imag_part = s * scaled * lax.rsqrt(rest)
    return real_part.astype(bf16), imag_part.astype(bf16)


def features(sites, is_source):
    x = sites.astype(f32)
    norm = jnp.sum(x * x, axis=0, keepdims=True)
    high = jnp.floor(norm * (1.0 / 256.0)) * 256.0
    low = norm - high
    one = jnp.ones_like(norm)
    if is_source:
        parts = [-2.0 * x, one, one, high, low, jnp.zeros_like(norm)]
    else:
        parts = [x, high, low, one, one, jnp.zeros_like(norm)]
    return jnp.concatenate(parts, 0)


def split(x):
    high = x.astype(bf16)
    return high, (x - high.astype(f32)).astype(bf16)


def stack(x):
    x_high, x_low = split(x)
    return jnp.concatenate([x_high.astype(f32), x_low.astype(f32)], 0).astype(bf16)


def times_i(x):
    half = x.shape[0] // 2
    return jnp.concatenate([-x[half:], x[:half]], 0)


def fold(x):
    half = x.shape[0] // 2
    return x[:half] + x[half:]


lanes = (((1,), (1,)), ((), ()))


def bit_of(x, size):
    return (x // size) % 2 if isinstance(x, int) else lax.rem(lax.div(x, size), 2)


def xor(a, b, n):
    out = 0
    size = 1
    while size < n:
        out = out + lax.rem(bit_of(a, size) + bit_of(b, size), 2) * size
        size *= 2
    return out


def position(R, C, G):
    row, col, grp = lax.axis_index("row"), lax.axis_index("col"), lax.axis_index("grp")
    me = col * G + grp
    rows = [row] + [xor(row, q, R) for q in range(1, R)]
    parts = [me] + [xor(me, s, C * G) for s in range(1, C * G)]
    return row, col, grp, me, rows, parts


def copy_to(src, dst, send, recv, device):
    return pltpu.make_async_remote_copy(
        src_ref=src, dst_ref=dst, send_sem=send, recv_sem=recv, device_id=device, device_id_type=MESH
    )


def source(gath, slot):
    block = gath[slot].astype(f32)
    half = block.shape[0] // 2
    sent = block[:half]
    both = jnp.concatenate([sent, times_i(sent)], 1).astype(bf16)
    sites = jnp.concatenate([block[half:], jnp.zeros_like(sent)], 0).T.astype(bf16)
    return sites, both


def pair(src, targets, masked=False):
    sites, both = src
    squared = jnp.dot(sites, targets, preferred_element_type=f32)
    real_part, imag_part = green(squared, masked)
    return jnp.dot(both, jnp.concatenate([real_part, imag_part], 0), preferred_element_type=f32)


def split_rows(basis, i, width, NB, ch):
    rows = jnp.concatenate(
        [
            jnp.concatenate(
                [basis[i * (width // 128) + v, pl.ds(c, NB, stride=ch), :] for v in range(width // 128)], 1
            )
            for c in range(ch)
        ], 0,
    )
    return split(rows)


def first_kernel(
    dims, table_hbm, basis_hbm, lattice_hbm, index_hbm, gath, tgt, partial, high, low, overlap,
    table_ref, direction, lattice_ref, index_ref, basis, copy_sem, send_g, recv_g,
):
    R, C, G, blk, points, nb, NB, ch, table = dims
    parts = C * G
    T = parts * blk
    K = nb * ch
    KP = NB * ch
    HK = KP // 2
    HG = HK // G
    row, col, grp, me, row_peer, part_peer = position(R, C, G)

    def at(part):
        return pl.ds(pl.multiple_of(part * blk, blk), blk)

    own = at(me)
    loads = [
        pltpu.make_async_copy(lattice_hbm, lattice_ref, copy_sem.at[0]),
        pltpu.make_async_copy(index_hbm.at[:, own], index_ref, copy_sem.at[1]),
        pltpu.make_async_copy(basis_hbm.at[pl.ds(K - ch, ch), own], direction, copy_sem.at[2]),
        pltpu.make_async_copy(table_hbm, table_ref, copy_sem.at[3]),
    ]
    for v in range(T // 128):
        loads.append(pltpu.make_async_copy(
            basis_hbm.at[:, pl.ds(v * 128, 128)], basis.at[v, pl.ds(0, K)], copy_sem.at[4 + v]
        ))
    for load in loads:
        load.start()
    barrier = pltpu.get_barrier_semaphore()
    for q in range(1, R):
        pl.semaphore_signal(barrier, inc=1, device_id={"row": row_peer[q]}, device_id_type=MESH)
    basis[:, K:] = jnp.zeros((T // 128, KP - K, 128), f32)
    for load in loads[:4]:
        load.wait()
    index = index_ref[...]
    strength = jnp.zeros(index.shape, f32)
    for entry in range(table):
        strength = jnp.where(index == entry, table_ref[entry], strength)
    own_sites = features(lattice_ref[:, own], True)
    gath[0] = jnp.concatenate([direction[...] * strength, own_sites], 0).astype(bf16)
    pl.semaphore_wait(barrier, R - 1)
    gathers = [None] + [
        copy_to(gath.at[0], gath.at[q], send_g.at[q], recv_g.at[q], {"row": row_peer[q]}) for q in range(1, R)
    ]
    for q in range(R - 1, 0, -1):
        gathers[q].start()
    zeros = jnp.zeros((8, T), f32)
    tgt[...] = jnp.concatenate([features(lattice_ref[...], False), zeros], 0).astype(bf16)
    mine = source(gath, 0)
    for s in range(parts):
        partial[pl.ds(part_peer[s], 1)] = pair(mine, tgt[:, at(part_peer[s])], s == 0)[None]
    for load in loads[4:]:
        load.wait()

    overlap[...] = jnp.zeros_like(overlap)
    real_rows = pl.ds(pl.multiple_of(grp * HG, HG), HG)
    imag_rows = pl.ds(pl.multiple_of(HK + grp * HG, HG), HG)

    @pl.loop(0, parts // 2)
    def _(i):
        left, right = [], []
        for k in range(2):
            cols = at(i * 2 + k)
            b_high, b_low = split_rows(basis, i * 2 + k, blk, NB, ch)
            high[:, cols] = b_high
            low[:, cols] = b_low
            kept = jnp.concatenate([high[real_rows, cols], high[imag_rows, cols]], 0)
            left += [kept, kept]
            right += [b_high * bf16(0.5), b_low]
        products = lax.dot_general(
            jnp.concatenate(left, 1), jnp.concatenate(right, 1), lanes, preferred_element_type=f32
        )
        overlap[0] += products[:HG, :HK] + products[HG:, HK:]
        overlap[1] += products[:HG, HK:] - products[HG:, :HK]

    for q in range(1, R):
        gathers[q].wait()


def kernel(
    dims, gath, tgt, begun, high, low, mine_ref, hess_ref, gram_ref, new_ref,
    overlap, metric, gram, partial, landed, field, near, far, *sems,
):
    R, C, G, blk, points, nb, NB, ch, table = dims
    parts = C * G
    T = parts * blk
    K = nb * ch
    half = ch // 2
    KP = NB * ch
    HK = NB * half
    HG = HK // G
    scale = 1.0 / points
    (send_h, recv_h, send_p, recv_p, send_f, recv_f, send_n, recv_n, send_z, recv_z,
     send_c, recv_c) = sems
    row, col, grp, me, row_peer, part_peer = position(R, C, G)

    def row_id(other):
        return {"row": other}

    def part_id(other):
        return {"col": lax.div(other, G), "grp": lax.rem(other, G)}

    def at(part):
        return pl.ds(pl.multiple_of(part * blk, blk), blk)

    own = at(me)
    barrier = pltpu.get_barrier_semaphore()
    for q in range(1, R):
        pl.semaphore_signal(barrier, inc=1, device_id=row_id(row_peer[q]), device_id_type=MESH)
    for s in range(1, parts):
        pl.semaphore_signal(barrier, inc=1, device_id=part_id(part_peer[s]), device_id_type=MESH)

    def metric_copy(slot, q):
        return copy_to(
            metric.at[slot], metric.at[slot], send_h.at[q], recv_h.at[slot], row_id(row_peer[q])
        )

    def share_copy(slot, k):
        return copy_to(
            gram.at[slot], gram.at[slot], send_c.at[k], recv_c.at[slot], {"grp": lax.rem(grp + k, G)}
        )

    def enter():
        pl.semaphore_wait(barrier, R - 1 + parts - 1)
        metric[pl.ds(row, 1)] = jnp.concatenate([mine_ref[0], mine_ref[1]], 1)[None]
        for q in range(R - 1, 0, -1):
            metric_copy(row, q).start()

    def part_copy(s):
        return copy_to(
            partial.at[part_peer[s]], landed.at[s], send_p.at[s], recv_p.at[s], part_id(part_peer[s])
        )

    def off_row(part, sources):
        total = begun[pl.ds(part, 1)][0]
        for src in sources:
            total = total + pair(src, tgt[:, at(part)])
        return total

    if (R - 1) * parts <= 32:
        sources = [source(gath, q) for q in range(1, R)]
        for first, last in ((parts - 1, parts // 2), (parts // 2 - 1, 1)):
            for s in range(first, last - 1, -1):
                partial[pl.ds(part_peer[s], 1)] = off_row(part_peer[s], sources)[None]
            if last > 1:
                enter()
            for s in range(first, last - 1, -1):
                part_copy(s).start()
        total = off_row(me, sources)
    else:
        enter()

        @pl.loop(0, parts - 1)
        def _(k):
            s = parts - 1 - k
            part = xor(me, s, parts)
            partial[pl.ds(part, 1)] = off_row(part, [source(gath, q) for q in range(1, R)])[None]
            copy_to(partial.at[part], landed.at[s], send_p.at[s], recv_p.at[s], part_id(part)).start()

        total = off_row(me, [source(gath, q) for q in range(1, R)])
    for s in range(parts - 1, 0, -1):
        part_copy(s).wait()
        total = total + landed[s]
    field[:, own] = total

    def field_copy(s, part):
        return copy_to(
            field.at[:, at(part)], field.at[:, at(part)], send_f.at[s], recv_f.at[s],
            part_id(part_peer[s]),
        )


    stacked = stack(total)
    raw = fold(lax.dot_general(
        jnp.concatenate([stacked, stacked], 1), jnp.concatenate([high[:, own], low[:, own]], 1),
        lanes, preferred_element_type=f32,
    ))
    norm = fold(lax.dot_general(stacked, stacked, lanes, preferred_element_type=f32))
    norm = norm[:, :ch] + norm[:, ch:]
    coef = raw[:, :HK] - times_i(raw[:, HK:])
    norm = norm[:, :half] - times_i(norm[:, half:])
    lane = lax.broadcasted_iota(jnp.int32, (ch, HK), 1)
    for a in range(half):
        coef = jnp.where(lane == a * NB + nb, norm[:, a:a + 1], coef)
    near[pl.ds(row, 1)] = coef[None]
    for q in range(R - 1, 0, -1):
        copy_to(near.at[row], near.at[row], send_n.at[q], recv_n.at[row], row_id(row_peer[q])).start()
    for s in range(parts - 1, 0, -1):
        field_copy(s, me).start()

    for q in range(1, R):
        metric_copy(row_peer[q], q).wait()
    gram[pl.ds(grp, 1)] = (jnp.sum(metric[...], 0) * scale)[None]
    for k in range(1, G):
        share_copy(grp, k).start()
    for q in range(1, R):
        peer = row_peer[q]
        copy_to(near.at[peer], near.at[peer], send_n.at[q], recv_n.at[peer], row_id(peer)).wait()
    far[pl.ds(me, 1)] = jnp.sum(near[...], 0)[None]
    for s in range(parts - 1, 0, -1):
        copy_to(far.at[me], far.at[me], send_z.at[s], recv_z.at[me], part_id(part_peer[s])).start()
    for s in range(1, parts):
        field_copy(s, part_peer[s]).wait()
    for k in range(1, G):
        share_copy(grp, k).wait_send()
        share_copy(lax.rem(grp + G - k, G), k).wait_recv()
    parts_of = jnp.concatenate([gram[k] for k in range(G)], 0)
    even, odd = parts_of[:, :HK], parts_of[:, HK:]
    full = jnp.concatenate([even + even.T, odd - odd.T], 1)
    full_high, full_low = split(full)
    full_both = jnp.concatenate([full_high, full_low], 0)
    overlap[0], overlap[1] = full[:, :HK], full[:, HK:]
    last = pl.ds(nb - 1, half, stride=NB)
    once = jnp.concatenate([overlap[0, last, :], -overlap[1, last, :]], 0)
    for s in range(1, parts):
        peer = part_peer[s]
        copy_to(far.at[peer], far.at[peer], send_z.at[s], recv_z.at[peer], part_id(peer)).wait()
    sums = jnp.sum(far[...], 0) * scale

    def apply(x):
        x16 = stack(x)
        y = fold(jnp.dot(jnp.concatenate([x16, x16], 1), full_both, preferred_element_type=f32))
        return y[:, :HK] - times_i(y[:, HK:])

    in_basis = lax.rem(lane, NB) < nb
    at_row = lax.broadcasted_iota(jnp.int32, (ch, HK), 0)
    mixed = jnp.where(in_basis, sums, 0.0)
    once = once - mixed
    both = 2.0 * once - apply(once)
    change = both - jnp.where(lane == at_row * NB + (nb - 1), 1.0, 0.0)
    lifted = stack(jnp.concatenate([change, times_i(change)], 1))
    for part in range(parts):
        cols = slice(part * blk, (part + 1) * blk)
        out = jnp.dot(lifted, high[:, cols], preferred_element_type=f32)
        out = out + jnp.dot(lifted, low[:, cols], preferred_element_type=f32)
        new_ref[:, cols] = -(field[:, cols] + fold(out))
    for i in range(2):
        for a in range(half):
            hess_ref[i, a] = both[i * half:(i + 1) * half, a * NB:a * NB + nb]
    other = mixed + apply(change)
    cross = fold(lax.dot_general(
        stack(jnp.concatenate([change, mixed], 1)), stack(jnp.concatenate([other, change], 1)),
        lanes, preferred_element_type=f32,
    ))
    cross = cross[:, :ch] + cross[:, ch:]
    self_gram = jnp.concatenate([sums[:, a * NB + nb:a * NB + nb + 1] for a in range(half)], 1)
    gram_ref[0] = self_gram[:half].T + cross[:half, :half] + cross[half:, half:]
    gram_ref[1] = self_gram[half:].T + cross[:half, half:] - cross[half:, :half]


def store(*refs):
    sem = refs[-1]
    copies = [pltpu.make_async_copy(refs[i], refs[3 + i], sem.at[i]) for i in (2, 0, 1)]
    for copy in copies:
        copy.start()
    for copy in copies:
        copy.wait()


def local(krylov_basis, lattice, strength_index, strength_table):
    R, C, G = (lax.axis_size(a) for a in ("row", "col", "grp"))
    nb, ch, T = krylov_basis.shape
    parts = C * G
    blk = T // parts
    K = nb * ch
    half = ch // 2
    NB = -(-(nb + 1) // 32) * 32
    KP, HK = NB * ch, NB * half
    table = strength_table.shape[0]
    dims = (R, C, G, blk, T * R, nb, NB, ch, table)
    vmem = pl.BlockSpec(memory_space=pltpu.VMEM)
    hbm = pl.BlockSpec(memory_space=pltpu.HBM)
    dma = pltpu.SemaphoreType.DMA
    begun = pl.pallas_call(
        functools.partial(first_kernel, dims),
        out_shape=(
            jax.ShapeDtypeStruct((R, 2 * ch, blk), bf16),
            jax.ShapeDtypeStruct((16, T), bf16),
            jax.ShapeDtypeStruct((parts, ch, blk), f32),
            jax.ShapeDtypeStruct((KP, T), bf16),
            jax.ShapeDtypeStruct((KP, T), bf16),
            jax.ShapeDtypeStruct((2, HK // G, HK), f32),
        ),
        in_specs=[hbm, hbm, hbm, hbm],
        out_specs=(vmem,) * 6,
        scratch_shapes=[
            pltpu.SMEM((table,), f32),
            pltpu.VMEM((ch, blk), f32),
            pltpu.VMEM((3, T), jnp.int32),
            pltpu.VMEM((1, blk), jnp.int32),
            pltpu.VMEM((T // 128, KP, 128), f32),
            dma((4 + T // 128,)),
            dma((R,)), dma((R,)),
        ],
        compiler_params=pltpu.CompilerParams(
            collective_id=0, has_side_effects=True, vmem_limit_bytes=25165824
        ),
        name="foldy_begin",
    )(*[pltpu.with_memory_space_constraint(v, pltpu.HBM) for v in (strength_table, krylov_basis.reshape(K, T), lattice, strength_index.reshape(1, T))])
    hess, gram, new_block = pl.pallas_call(
        functools.partial(kernel, dims),
        out_shape=(
            jax.ShapeDtypeStruct((2, half, half, nb), f32),
            jax.ShapeDtypeStruct((2, half, half), f32),
            jax.ShapeDtypeStruct((ch, T), f32),
        ),
        in_specs=[vmem] * 6,
        out_specs=(vmem, vmem, vmem),
        scratch_shapes=[
            pltpu.VMEM((2, HK, HK), f32),
            pltpu.VMEM((R, HK // G, 2 * HK), f32),
            pltpu.VMEM((G, HK // G, 2 * HK), f32),
            pltpu.VMEM((parts, ch, blk), f32),
            pltpu.VMEM((parts, ch, blk), f32),
            pltpu.VMEM((ch, T), f32),
            pltpu.VMEM((R, ch, HK), f32),
            pltpu.VMEM((parts, ch, HK), f32),
            dma((R,)), dma((R,)),
            dma((parts,)), dma((parts,)),
            dma((parts,)), dma((parts,)),
            dma((R,)), dma((R,)),
            dma((parts,)), dma((parts,)),
            dma((G,)), dma((G,)),
        ],
        compiler_params=pltpu.CompilerParams(
            collective_id=1, has_side_effects=True, vmem_limit_bytes=25165824
        ),
        name="foldy_step",
    )(*begun)
    hess, gram, new_block = pl.pallas_call(
        store,
        out_shape=tuple(jax.ShapeDtypeStruct(v.shape, v.dtype) for v in (hess, gram, new_block)),
        in_specs=[vmem, vmem, vmem],
        out_specs=(hbm, hbm, hbm),
        scratch_shapes=[dma((3,))],
        compiler_params=pltpu.CompilerParams(vmem_limit_bytes=1048576),
        name="store",
    )(hess, gram, new_block)
    return (new_block, hess.transpose(3, 0, 1, 2), gram)


def solution(mesh):
    in_specs = (P(None, None, "row"), P(None, "row"), P("row"), P())
    out_specs = (P(None, "row"), P(), P())
    return jax.shard_map(local, mesh=mesh, in_specs=in_specs, out_specs=out_specs, check_vma=False)
```

time: 27.9 us -> 26.2 us (0.939)
  local copies, waits for them, and re-layouts: 1.83 us -> 0 us
    pallas_call x0 -> x2, Pallas kernels: none -> 8.58 us  [the longest x1 7.92 us: local(): pl.pallas_call(functools.partial(first_kernel, dims), out_shape=(jax.Shap...]
    pallas_call x1, Pallas kernels: 25.3 us -> 16.8 us  [local(): pl.pallas_call(functools.partial(kernel, dims), out_shape=(jax.ShapeDtype...]
    unnamed x3 -> x0, local copies, waits for them, and re-layouts: 1.83 us -> none
where the time goes in v2:
time: 26.2 us; the launch traced here: 26 us
  Pallas kernels  25.4 us (97%)
  between operations  0.65 us (2%)
    pallas_call x1, Pallas kernels, local(): pl.pallas_call(functools.partial(kernel, dims), out_shape=(jax.ShapeDtype...  16.8 us
    pallas_call x1, Pallas kernels, local(): pl.pallas_call(functools.partial(first_kernel, dims), out_shape=(jax.Shap...  7.92 us
    pallas_call x1, Pallas kernels, local(): pl.pallas_call(store, out_shape=tuple((jax.ShapeDtypeStruct(v.shape, v.dt...  0.66 us

profile of v2, /device:TPU:0, one launch (start us, length us, event | category | flops | bytes accessed | tf_op | source)
XLA Modules:
  0.0 26.0 jit_solution(2610878136711329637)
XLA Ops:
  0.6 7.9 %foldy_begin.1 = (bf16[4,16,256]{2,1,0:T(8,128)(2,1)S(1)}, bf16[16,2048]{1,0:T(8,128)(2,1)S(1)}, f32[8,8,256]{2,1,0:T(8,128)S(1)}, bf16[256,2048]{1,0:T(8,128)(2...) custom-call(f32[16]{0:T(128)} %table_hbm.1, f32[240,2048]{1,0:T(8,128)} %bitcast.3, ...), custom_call_target="tpu_custom_call" | custom-call | tf_op jit(solution)/shard_map/foldy_begin/pallas_call | solution.py:403
  8.6 16.8 %foldy_step.1 = (f32[2,4,4,30]{3,2,1,0:T(4,128)S(1)}, f32[2,4,4]{2,1,0:T(4,128)S(1)}, f32[8,2048]{1,0:T(8,128)S(1)}) custom-call(bf16[4,16,256]{2,1,0:T(8,128)(2,1)S(1)} %get-tuple-element.15.gath, bf16[16,2048]{1,0:T(8,128)(2,1)S(1)} %get-tuple-element.16.tgt, f32[8,8,256]{2,1,0:T(8,128)S(1)} %get-tuple-element.17.begun, ...), custom_call_target="tpu_custom_call" | custom-call | tf_op jit(solution)/shard_map/foldy_step/pallas_call | solution.py:429
  25.3 0.7 %store.1 = (f32[2,4,4,30]{3,2,1,0:T(4,128)}, f32[2,4,4]{2,1,0:T(4,128)}, f32[8,2048]{1,0:T(8,128)}) custom-call(f32[2,4,4,30]{3,2,1,0:T(4,128)S(1)} %get-tuple-element.21.refs_0_, f32[2,4,4]{2,1,0:T(4,128)S(1)} %get-tuple-element.22.refs_1_, f32[8,2048]{1,0:T(8,128)S(1)} %get-tuple-element.23.refs_2_), custom_call_target="tpu_custom_call" | custom-call | tf_op jit(solution)/shard_map/store/pallas_call | solution.py:459

commit v3 on v2

--- a/solution.py
+++ b/solution.py
@@ -233,9 +233,14 @@
         return pl.ds(pl.multiple_of(part * blk, blk), blk)
 
     own = at(me)
+    core_peer = [grp] + [xor(grp, k, G) for k in range(1, G)]
+    col_peer = [col] + [xor(col, z, C) for z in range(1, C)]
     barrier = pltpu.get_barrier_semaphore()
     for q in range(1, R):
-        pl.semaphore_signal(barrier, inc=1, device_id=row_id(row_peer[q]), device_id_type=MESH)
+        for k in range(G):
+            pl.semaphore_signal(
+                barrier, inc=1, device_id={"row": row_peer[q], "grp": core_peer[k]}, device_id_type=MESH
+            )
     for s in range(1, parts):
         pl.semaphore_signal(barrier, inc=1, device_id=part_id(part_peer[s]), device_id_type=MESH)
 
@@ -250,7 +255,7 @@
         )
 
     def enter():
-        pl.semaphore_wait(barrier, R - 1 + parts - 1)
+        pl.semaphore_wait(barrier, (R - 1) * G + parts - 1)
         metric[pl.ds(row, 1)] = jnp.concatenate([mine_ref[0], mine_ref[1]], 1)[None]
         for q in range(R - 1, 0, -1):
             metric_copy(row, q).start()
@@ -268,12 +273,12 @@
 
     if (R - 1) * parts <= 32:
         sources = [source(gath, q) for q in range(1, R)]
-        for first, last in ((parts - 1, parts // 2), (parts // 2 - 1, 1)):
-            for s in range(first, last - 1, -1):
+        for batch, leaving in enumerate((range(parts - 1, parts // 2 - 1, -1), range(parts // 2 - 1, 1, -1), (1,))):
+            for s in leaving:
                 partial[pl.ds(part_peer[s], 1)] = off_row(part_peer[s], sources)[None]
-            if last > 1:
+            if batch == 0:
                 enter()
-            for s in range(first, last - 1, -1):
+            for s in leaving:
                 part_copy(s).start()
         total = off_row(me, sources)
     else:
@@ -311,9 +316,14 @@
     lane = lax.broadcasted_iota(jnp.int32, (ch, HK), 1)
     for a in range(half):
         coef = jnp.where(lane == a * NB + nb, norm[:, a:a + 1], coef)
-    near[pl.ds(row, 1)] = coef[None]
-    for q in range(R - 1, 0, -1):
-        copy_to(near.at[row], near.at[row], send_n.at[q], recv_n.at[row], row_id(row_peer[q])).start()
+    plane = [
+        (row_peer[q] * G + core_peer[k], {"row": row_peer[q], "grp": core_peer[k]}, q * G + k)
+        for q in range(R) for k in range(G)
+    ]
+    here = row * G + grp
+    near[pl.ds(here, 1)] = coef[None]
+    for slot, device, index in plane[:0:-1]:
+        copy_to(near.at[here], near.at[here], send_n.at[index], recv_n.at[here], device).start()
     for s in range(parts - 1, 0, -1):
         field_copy(s, me).start()
 
@@ -322,12 +332,11 @@
     gram[pl.ds(grp, 1)] = (jnp.sum(metric[...], 0) * scale)[None]
     for k in range(1, G):
         share_copy(grp, k).start()
-    for q in range(1, R):
-        peer = row_peer[q]
-        copy_to(near.at[peer], near.at[peer], send_n.at[q], recv_n.at[peer], row_id(peer)).wait()
-    far[pl.ds(me, 1)] = jnp.sum(near[...], 0)[None]
-    for s in range(parts - 1, 0, -1):
-        copy_to(far.at[me], far.at[me], send_z.at[s], recv_z.at[me], part_id(part_peer[s])).start()
+    for slot, device, index in plane[1:]:
+        copy_to(near.at[slot], near.at[slot], send_n.at[index], recv_n.at[slot], device).wait()
+    far[pl.ds(col, 1)] = jnp.sum(near[...], 0)[None]
+    for z in range(C - 1, 0, -1):
+        copy_to(far.at[col], far.at[col], send_z.at[z], recv_z.at[col], {"col": col_peer[z]}).start()
     for s in range(1, parts):
         field_copy(s, part_peer[s]).wait()
     for k in range(1, G):
@@ -341,9 +350,9 @@
     overlap[0], overlap[1] = full[:, :HK], full[:, HK:]
     last = pl.ds(nb - 1, half, stride=NB)
     once = jnp.concatenate([overlap[0, last, :], -overlap[1, last, :]], 0)
-    for s in range(1, parts):
-        peer = part_peer[s]
-        copy_to(far.at[peer], far.at[peer], send_z.at[s], recv_z.at[peer], part_id(peer)).wait()
+    for z in range(1, C):
+        peer = col_peer[z]
+        copy_to(far.at[peer], far.at[peer], send_z.at[z], recv_z.at[peer], {"col": peer}).wait()
     sums = jnp.sum(far[...], 0) * scale
 
     def apply(x):
@@ -442,13 +451,13 @@
             pltpu.VMEM((parts, ch, blk), f32),
             pltpu.VMEM((parts, ch, blk), f32),
             pltpu.VMEM((ch, T), f32),
-            pltpu.VMEM((R, ch, HK), f32),
-            pltpu.VMEM((parts, ch, HK), f32),
+            pltpu.VMEM((R * G, ch, HK), f32),
+            pltpu.VMEM((C, ch, HK), f32),
             dma((R,)), dma((R,)),
             dma((parts,)), dma((parts,)),
             dma((parts,)), dma((parts,)),
-            dma((R,)), dma((R,)),
-            dma((parts,)), dma((parts,)),
+            dma((R * G,)), dma((R * G,)),
+            dma((C,)), dma((C,)),
             dma((G,)), dma((G,)),
         ],
         compiler_params=pltpu.CompilerParams(

time: 26.2 us -> 25.5 us (0.973)
  Pallas kernels: 25.4 us -> 24.7 us
    pallas_call x1, Pallas kernels: 16.8 us -> 16.1 us  [local(): pl.pallas_call(functools.partial(kernel, dims), out_shape=(jax.ShapeDtype...]
where the time goes in v3:
time: 25.5 us; the launch traced here: 25.4 us
  Pallas kernels  24.7 us (97%)
  between operations  0.65 us (3%)
    pallas_call x1, Pallas kernels, local(): pl.pallas_call(functools.partial(kernel, dims), out_shape=(jax.ShapeDtype...  16.1 us
    pallas_call x1, Pallas kernels, local(): pl.pallas_call(functools.partial(first_kernel, dims), out_shape=(jax.Shap...  7.92 us
    pallas_call x1, Pallas kernels, local(): pl.pallas_call(store, out_shape=tuple((jax.ShapeDtypeStruct(v.shape, v.dt...  0.66 us

profile of v3, /device:TPU:0, one launch (start us, length us, event | category | flops | bytes accessed | tf_op | source)
XLA Modules:
  0.0 25.4 jit_solution(5825368423154270622)
XLA Ops:
  0.6 7.9 %foldy_begin.1 = (bf16[4,16,256]{2,1,0:T(8,128)(2,1)S(1)}, bf16[16,2048]{1,0:T(8,128)(2,1)S(1)}, f32[8,8,256]{2,1,0:T(8,128)S(1)}, bf16[256,2048]{1,0:T(8,128)(2...) custom-call(f32[16]{0:T(128)} %table_hbm.1, f32[240,2048]{1,0:T(8,128)} %bitcast.3, ...), custom_call_target="tpu_custom_call" | custom-call | tf_op jit(solution)/shard_map/foldy_begin/pallas_call | solution.py:412
  8.6 16.1 %foldy_step.1 = (f32[2,4,4,30]{3,2,1,0:T(4,128)S(1)}, f32[2,4,4]{2,1,0:T(4,128)S(1)}, f32[8,2048]{1,0:T(8,128)S(1)}) custom-call(bf16[4,16,256]{2,1,0:T(8,128)(2,1)S(1)} %get-tuple-element.15.gath, bf16[16,2048]{1,0:T(8,128)(2,1)S(1)} %get-tuple-element.16.tgt, f32[8,8,256]{2,1,0:T(8,128)S(1)} %get-tuple-element.17.begun, ...), custom_call_target="tpu_custom_call" | custom-call | tf_op jit(solution)/shard_map/foldy_step/pallas_call | solution.py:438
  24.7 0.7 %store.1 = (f32[2,4,4,30]{3,2,1,0:T(4,128)}, f32[2,4,4]{2,1,0:T(4,128)}, f32[8,2048]{1,0:T(8,128)}) custom-call(f32[2,4,4,30]{3,2,1,0:T(4,128)S(1)} %get-tuple-element.21.refs_0_, f32[2,4,4]{2,1,0:T(4,128)S(1)} %get-tuple-element.22.refs_1_, f32[8,2048]{1,0:T(8,128)S(1)} %get-tuple-element.23.refs_2_), custom_call_target="tpu_custom_call" | custom-call | tf_op jit(solution)/shard_map/store/pallas_call | solution.py:468

commit v4 on v3

--- a/solution.py
+++ b/solution.py
@@ -207,8 +207,8 @@
 
 
 def kernel(
-    dims, gath, tgt, begun, high, low, mine_ref, hess_ref, gram_ref, new_ref,
-    overlap, metric, gram, partial, landed, field, near, far, *sems,
+    dims, gath, tgt, begun, high, low, mine_ref, sums_ref, once_ref, full_ref, field,
+    overlap, metric, gram, partial, landed, near, far, *sems,
 ):
     R, C, G, blk, points, nb, NB, ch, table = dims
     parts = C * G
@@ -304,6 +304,8 @@
         )
 
 
+    for s in range(parts - 1, 0, -1):
+        field_copy(s, me).start()
     stacked = stack(total)
     raw = fold(lax.dot_general(
         jnp.concatenate([stacked, stacked], 1), jnp.concatenate([high[:, own], low[:, own]], 1),
@@ -324,8 +326,6 @@
     near[pl.ds(here, 1)] = coef[None]
     for slot, device, index in plane[:0:-1]:
         copy_to(near.at[here], near.at[here], send_n.at[index], recv_n.at[here], device).start()
-    for s in range(parts - 1, 0, -1):
-        field_copy(s, me).start()
 
     for q in range(1, R):
         metric_copy(row_peer[q], q).wait()
@@ -346,15 +346,26 @@
     even, odd = parts_of[:, :HK], parts_of[:, HK:]
     full = jnp.concatenate([even + even.T, odd - odd.T], 1)
     full_high, full_low = split(full)
-    full_both = jnp.concatenate([full_high, full_low], 0)
+    full_ref[...] = jnp.concatenate([full_high, full_low], 0)
     overlap[0], overlap[1] = full[:, :HK], full[:, HK:]
     last = pl.ds(nb - 1, half, stride=NB)
-    once = jnp.concatenate([overlap[0, last, :], -overlap[1, last, :]], 0)
+    once_ref[...] = jnp.concatenate([overlap[0, last, :], -overlap[1, last, :]], 0)
     for z in range(1, C):
         peer = col_peer[z]
         copy_to(far.at[peer], far.at[peer], send_z.at[z], recv_z.at[peer], {"col": peer}).wait()
-    sums = jnp.sum(far[...], 0) * scale
-
+    sums_ref[...] = jnp.sum(far[...], 0) * scale
+
+
+def finish(
+    dims, sums_ref, once_ref, full_ref, field, high, low, hess_hbm, gram_hbm, new_hbm,
+    hess_ref, gram_ref, new_ref, sem,
+):
+    R, C, G, blk, points, nb, NB, ch, table = dims
+    parts = C * G
+    half = ch // 2
+    HK = NB * half
+    sums, once, full_both = sums_ref[...], once_ref[...], full_ref[...]
+    lane = lax.broadcasted_iota(jnp.int32, (ch, HK), 1)
     def apply(x):
         x16 = stack(x)
         y = fold(jnp.dot(jnp.concatenate([x16, x16], 1), full_both, preferred_element_type=f32))
@@ -367,31 +378,39 @@
     both = 2.0 * once - apply(once)
     change = both - jnp.where(lane == at_row * NB + (nb - 1), 1.0, 0.0)
     lifted = stack(jnp.concatenate([change, times_i(change)], 1))
+    sent = []
+
+    def put(src, dst):
+        sent.append(pltpu.make_async_copy(src, dst, sem.at[len(sent)]))
+        sent[-1].start()
+
+    for i in range(2):
+        for a in range(half):
+            hess_ref[i, a] = both[i * half:(i + 1) * half, a * NB:a * NB + nb]
+    self_gram = jnp.concatenate([sums[:, a * NB + nb:a * NB + nb + 1] for a in range(half)], 1)
     for part in range(parts):
         cols = slice(part * blk, (part + 1) * blk)
         out = jnp.dot(lifted, high[:, cols], preferred_element_type=f32)
         out = out + jnp.dot(lifted, low[:, cols], preferred_element_type=f32)
         new_ref[:, cols] = -(field[:, cols] + fold(out))
-    for i in range(2):
-        for a in range(half):
-            hess_ref[i, a] = both[i * half:(i + 1) * half, a * NB:a * NB + nb]
-    other = mixed + apply(change)
-    cross = fold(lax.dot_general(
-        stack(jnp.concatenate([change, mixed], 1)), stack(jnp.concatenate([other, change], 1)),
-        lanes, preferred_element_type=f32,
-    ))
-    cross = cross[:, :ch] + cross[:, ch:]
-    self_gram = jnp.concatenate([sums[:, a * NB + nb:a * NB + nb + 1] for a in range(half)], 1)
-    gram_ref[0] = self_gram[:half].T + cross[:half, :half] + cross[half:, half:]
-    gram_ref[1] = self_gram[half:].T + cross[:half, half:] - cross[half:, :half]
-
-
-def store(*refs):
-    sem = refs[-1]
-    copies = [pltpu.make_async_copy(refs[i], refs[3 + i], sem.at[i]) for i in (2, 0, 1)]
-    for copy in copies:
-        copy.start()
-    for copy in copies:
+        if part == 0:
+            other = mixed + apply(change)
+        if part == 2:
+            cross = fold(lax.dot_general(
+                stack(jnp.concatenate([change, mixed], 1)), stack(jnp.concatenate([other, change], 1)),
+                lanes, preferred_element_type=f32,
+            ))
+            cross = cross[:, :ch] + cross[:, ch:]
+        if part == 3:
+            gram_ref[0] = self_gram[:half].T + cross[:half, :half] + cross[half:, half:]
+            gram_ref[1] = self_gram[half:].T + cross[:half, half:] - cross[half:, :half]
+        if part % 2:
+            cols = pl.ds((part - 1) * blk, 2 * blk)
+            put(new_ref.at[:, cols], new_hbm.at[:, cols])
+        if part == 3:
+            put(hess_ref, hess_hbm)
+            put(gram_ref, gram_hbm)
+    for copy in sent:
         copy.wait()
 
 
@@ -435,22 +454,22 @@
         ),
         name="foldy_begin",
     )(*[pltpu.with_memory_space_constraint(v, pltpu.HBM) for v in (strength_table, krylov_basis.reshape(K, T), lattice, strength_index.reshape(1, T))])
-    hess, gram, new_block = pl.pallas_call(
+    ended = pl.pallas_call(
         functools.partial(kernel, dims),
         out_shape=(
-            jax.ShapeDtypeStruct((2, half, half, nb), f32),
-            jax.ShapeDtypeStruct((2, half, half), f32),
+            jax.ShapeDtypeStruct((ch, HK), f32),
+            jax.ShapeDtypeStruct((ch, HK), f32),
+            jax.ShapeDtypeStruct((2 * HK, 2 * HK), bf16),
             jax.ShapeDtypeStruct((ch, T), f32),
         ),
         in_specs=[vmem] * 6,
-        out_specs=(vmem, vmem, vmem),
+        out_specs=(vmem,) * 4,
         scratch_shapes=[
             pltpu.VMEM((2, HK, HK), f32),
             pltpu.VMEM((R, HK // G, 2 * HK), f32),
             pltpu.VMEM((G, HK // G, 2 * HK), f32),
             pltpu.VMEM((parts, ch, blk), f32),
             pltpu.VMEM((parts, ch, blk), f32),
-            pltpu.VMEM((ch, T), f32),
             pltpu.VMEM((R * G, ch, HK), f32),
             pltpu.VMEM((C, ch, HK), f32),
             dma((R,)), dma((R,)),
@@ -465,15 +484,20 @@
         ),
         name="foldy_step",
     )(*begun)
+    outs = (
+        jax.ShapeDtypeStruct((2, half, half, nb), f32),
+        jax.ShapeDtypeStruct((2, half, half), f32),
+        jax.ShapeDtypeStruct((ch, T), f32),
+    )
     hess, gram, new_block = pl.pallas_call(
-        store,
-        out_shape=tuple(jax.ShapeDtypeStruct(v.shape, v.dtype) for v in (hess, gram, new_block)),
-        in_specs=[vmem, vmem, vmem],
-        out_specs=(hbm, hbm, hbm),
-        scratch_shapes=[dma((3,))],
-        compiler_params=pltpu.CompilerParams(vmem_limit_bytes=1048576),
-        name="store",
-    )(hess, gram, new_block)
+        functools.partial(finish, dims),
+        out_shape=outs,
+        in_specs=[vmem] * 6,
+        out_specs=(hbm,) * 3,
+        scratch_shapes=[pltpu.VMEM(v.shape, v.dtype) for v in outs] + [dma((parts // 2 + 2,))],
+        compiler_params=pltpu.CompilerParams(vmem_limit_bytes=8388608),
+        name="foldy_end",
+    )(*ended, begun[3], begun[4])
     return (new_block, hess.transpose(3, 0, 1, 2), gram)
 
 

time: 25.5 us -> 25.3 us (level)
    pallas_call x1, Pallas kernels: 16.1 us -> 15.3 us  [local(): pl.pallas_call(functools.partial(kernel, dims), out_shape=(jax.ShapeDtype...]
    pallas_call x1, Pallas kernels: 0.66 us -> 1.27 us  [local(): pl.pallas_call(functools.partial(finish, dims), out_shape=outs, in_specs=...]
where the time goes in v4:
time: 25.3 us; the launch traced here: 25.2 us
  Pallas kernels  24.5 us (97%)
  between operations  0.65 us (3%)
    pallas_call x1, Pallas kernels, local(): pl.pallas_call(functools.partial(kernel, dims), out_shape=(jax.ShapeDtype...  15.3 us
    pallas_call x1, Pallas kernels, local(): pl.pallas_call(functools.partial(first_kernel, dims), out_shape=(jax.Shap...  7.92 us
    pallas_call x1, Pallas kernels, local(): pl.pallas_call(functools.partial(finish, dims), out_shape=outs, in_specs=...  1.27 us

profile of v4, /device:TPU:0, one launch (start us, length us, event | category | flops | bytes accessed | tf_op | source)
XLA Modules:
  0.0 25.2 jit_solution(3401179918933866035)
XLA Ops:
  0.6 7.9 %foldy_begin.1 = (bf16[4,16,256]{2,1,0:T(8,128)(2,1)S(1)}, bf16[16,2048]{1,0:T(8,128)(2,1)S(1)}, f32[8,8,256]{2,1,0:T(8,128)S(1)}, bf16[256,2048]{1,0:T(8,128)(2...) custom-call(f32[16]{0:T(128)} %table_hbm.1, f32[240,2048]{1,0:T(8,128)} %bitcast.3, ...), custom_call_target="tpu_custom_call" | custom-call | tf_op jit(solution)/shard_map/foldy_begin/pallas_call | solution.py:431
  8.6 15.3 %foldy_step.1 = (f32[8,128]{1,0:T(8,128)S(1)}, f32[8,128]{1,0:T(8,128)S(1)}, bf16[256,256]{1,0:T(8,128)(2,1)S(1)}, f32[8,2048]{1,0:T(8,128)S(1)}) custom-call(bf16[4,16,256]{2,1,0:T(8,128)(2,1)S(1)} %get-tuple-element.16.gath, bf16[16,2048]{1,0:T(8,128)(2,1)S(1)} %get-tuple-element.17.tgt, f32[8,8,256]{2,1,0:T(8,128)S(1)} %get-tuple-element.18.begun, ...), custom_call_target="tpu_custom_call" | custom-call | tf_op jit(solution)/shard_map/foldy_step/pallas_call | solution.py:457
  23.9 1.3 %foldy_end.1 = (f32[2,4,4,30]{3,2,1,0:T(4,128)}, f32[2,4,4]{2,1,0:T(4,128)}, f32[8,2048]{1,0:T(8,128)}) custom-call(f32[8,128]{1,0:T(8,128)S(1)} %get-tuple-element.22.sums_ref, f32[8,128]{1,0:T(8,128)S(1)} %get-tuple-element.23.once_ref, bf16[256,256]{1,0:T(8,128)(2,1)S(1)} %get-tuple-element.24.full_ref, f32[8,2048]{1,0:T(8,128)S(1)} %get-tuple-element.25.field, ...), custom_call_target="tpu_custom_call" | custom-call | tf_op jit(solution)/shard_map/foldy_end/pallas_call | solution.py:492

commit v5 on v4

--- a/solution.py
+++ b/solution.py
@@ -181,16 +181,15 @@
     for load in loads[4:]:
         load.wait()
 
-    overlap[...] = jnp.zeros_like(overlap)
     real_rows = pl.ds(pl.multiple_of(grp * HG, HG), HG)
     imag_rows = pl.ds(pl.multiple_of(HK + grp * HG, HG), HG)
-
-    @pl.loop(0, parts // 2)
-    def _(i):
+    each = 4
+
+    def rows_of_gram(i):
         left, right = [], []
-        for k in range(2):
-            cols = at(i * 2 + k)
-            b_high, b_low = split_rows(basis, i * 2 + k, blk, NB, ch)
+        for k in range(each):
+            cols = at(i * each + k)
+            b_high, b_low = split_rows(basis, i * each + k, blk, NB, ch)
             high[:, cols] = b_high
             low[:, cols] = b_low
             kept = jnp.concatenate([high[real_rows, cols], high[imag_rows, cols]], 0)
@@ -199,8 +198,15 @@
         products = lax.dot_general(
             jnp.concatenate(left, 1), jnp.concatenate(right, 1), lanes, preferred_element_type=f32
         )
-        overlap[0] += products[:HG, :HK] + products[HG:, HK:]
-        overlap[1] += products[:HG, HK:] - products[HG:, :HK]
+        return products[:HG, :HK] + products[HG:, HK:], products[:HG, HK:] - products[HG:, :HK]
+
+    overlap[...] = jnp.zeros_like(overlap)
+
+    @pl.loop(0, parts // each)
+    def _(i):
+        even, odd = rows_of_gram(i)
+        overlap[0] += even
+        overlap[1] += odd
 
     for q in range(1, R):
         gathers[q].wait()

time: 25.3 us -> 25.3 us (level)
    pallas_call x1, Pallas kernels: 15.3 us -> 15.7 us  [local(): pl.pallas_call(functools.partial(kernel, dims), out_shape=(jax.ShapeDtype...]
    pallas_call x1, Pallas kernels: 7.92 us -> 7.58 us  [local(): pl.pallas_call(functools.partial(first_kernel, dims), out_shape=(jax.Shap...]
where the time goes in v5:
time: 25.3 us; the launch traced here: 25.2 us
  Pallas kernels  24.5 us (97%)
  between operations  0.65 us (3%)
    pallas_call x1, Pallas kernels, local(): pl.pallas_call(functools.partial(kernel, dims), out_shape=(jax.ShapeDtype...  15.7 us
    pallas_call x1, Pallas kernels, local(): pl.pallas_call(functools.partial(first_kernel, dims), out_shape=(jax.Shap...  7.58 us
    pallas_call x1, Pallas kernels, local(): pl.pallas_call(functools.partial(finish, dims), out_shape=outs, in_specs=...  1.27 us

profile of v5, /device:TPU:0, one launch (start us, length us, event | category | flops | bytes accessed | tf_op | source)
XLA Modules:
  0.0 25.2 jit_solution(9490331845804923242)
XLA Ops:
  0.6 7.6 %foldy_begin.1 = (bf16[4,16,256]{2,1,0:T(8,128)(2,1)S(1)}, bf16[16,2048]{1,0:T(8,128)(2,1)S(1)}, f32[8,8,256]{2,1,0:T(8,128)S(1)}, bf16[256,2048]{1,0:T(8,128)(2...) custom-call(f32[16]{0:T(128)} %table_hbm.1, f32[240,2048]{1,0:T(8,128)} %bitcast.3, ...), custom_call_target="tpu_custom_call" | custom-call | tf_op jit(solution)/shard_map/foldy_begin/pallas_call | solution.py:437
  8.2 15.7 %foldy_step.1 = (f32[8,128]{1,0:T(8,128)S(1)}, f32[8,128]{1,0:T(8,128)S(1)}, bf16[256,256]{1,0:T(8,128)(2,1)S(1)}, f32[8,2048]{1,0:T(8,128)S(1)}) custom-call(bf16[4,16,256]{2,1,0:T(8,128)(2,1)S(1)} %get-tuple-element.16.gath, bf16[16,2048]{1,0:T(8,128)(2,1)S(1)} %get-tuple-element.17.tgt, f32[8,8,256]{2,1,0:T(8,128)S(1)} %get-tuple-element.18.begun, ...), custom_call_target="tpu_custom_call" | custom-call | tf_op jit(solution)/shard_map/foldy_step/pallas_call | solution.py:463
  23.9 1.3 %foldy_end.1 = (f32[2,4,4,30]{3,2,1,0:T(4,128)}, f32[2,4,4]{2,1,0:T(4,128)}, f32[8,2048]{1,0:T(8,128)}) custom-call(f32[8,128]{1,0:T(8,128)S(1)} %get-tuple-element.22.sums_ref, f32[8,128]{1,0:T(8,128)S(1)} %get-tuple-element.23.once_ref, bf16[256,256]{1,0:T(8,128)(2,1)S(1)} %get-tuple-element.24.full_ref, f32[8,2048]{1,0:T(8,128)S(1)} %get-tuple-element.25.field, ...), custom_call_target="tpu_custom_call" | custom-call | tf_op jit(solution)/shard_map/foldy_end/pallas_call | solution.py:498

commit v6 on v5

--- a/solution.py
+++ b/solution.py
@@ -333,16 +333,16 @@
     for slot, device, index in plane[:0:-1]:
         copy_to(near.at[here], near.at[here], send_n.at[index], recv_n.at[here], device).start()
 
+    for slot, device, index in plane[1:]:
+        copy_to(near.at[slot], near.at[slot], send_n.at[index], recv_n.at[slot], device).wait()
+    far[pl.ds(col, 1)] = jnp.sum(near[...], 0)[None]
+    for z in range(C - 1, 0, -1):
+        copy_to(far.at[col], far.at[col], send_z.at[z], recv_z.at[col], {"col": col_peer[z]}).start()
     for q in range(1, R):
         metric_copy(row_peer[q], q).wait()
     gram[pl.ds(grp, 1)] = (jnp.sum(metric[...], 0) * scale)[None]
     for k in range(1, G):
         share_copy(grp, k).start()
-    for slot, device, index in plane[1:]:
-        copy_to(near.at[slot], near.at[slot], send_n.at[index], recv_n.at[slot], device).wait()
-    far[pl.ds(col, 1)] = jnp.sum(near[...], 0)[None]
-    for z in range(C - 1, 0, -1):
-        copy_to(far.at[col], far.at[col], send_z.at[z], recv_z.at[col], {"col": col_peer[z]}).start()
     for s in range(1, parts):
         field_copy(s, part_peer[s]).wait()
     for k in range(1, G):

time: 25.3 us -> 25.3 us (level)
  no operation moved by 1% of the time
where the time goes in v6:
time: 25.3 us; the launch traced here: 25.2 us
  Pallas kernels  24.5 us (97%)
  between operations  0.65 us (3%)
    pallas_call x1, Pallas kernels, local(): pl.pallas_call(functools.partial(kernel, dims), out_shape=(jax.ShapeDtype...  15.7 us
    pallas_call x1, Pallas kernels, local(): pl.pallas_call(functools.partial(first_kernel, dims), out_shape=(jax.Shap...  7.58 us
    pallas_call x1, Pallas kernels, local(): pl.pallas_call(functools.partial(finish, dims), out_shape=outs, in_specs=...  1.27 us

profile of v6, /device:TPU:0, one launch (start us, length us, event | category | flops | bytes accessed | tf_op | source)
XLA Modules:
  0.0 25.2 jit_solution(7268312301564596027)
XLA Ops:
  0.6 7.6 %foldy_begin.1 = (bf16[4,16,256]{2,1,0:T(8,128)(2,1)S(1)}, bf16[16,2048]{1,0:T(8,128)(2,1)S(1)}, f32[8,8,256]{2,1,0:T(8,128)S(1)}, bf16[256,2048]{1,0:T(8,128)(2...) custom-call(f32[16]{0:T(128)} %table_hbm.1, f32[240,2048]{1,0:T(8,128)} %bitcast.3, ...), custom_call_target="tpu_custom_call" | custom-call | tf_op jit(solution)/shard_map/foldy_begin/pallas_call | solution.py:437
  8.2 15.7 %foldy_step.1 = (f32[8,128]{1,0:T(8,128)S(1)}, f32[8,128]{1,0:T(8,128)S(1)}, bf16[256,256]{1,0:T(8,128)(2,1)S(1)}, f32[8,2048]{1,0:T(8,128)S(1)}) custom-call(bf16[4,16,256]{2,1,0:T(8,128)(2,1)S(1)} %get-tuple-element.16.gath, bf16[16,2048]{1,0:T(8,128)(2,1)S(1)} %get-tuple-element.17.tgt, f32[8,8,256]{2,1,0:T(8,128)S(1)} %get-tuple-element.18.begun, ...), custom_call_target="tpu_custom_call" | custom-call | tf_op jit(solution)/shard_map/foldy_step/pallas_call | solution.py:463
  23.9 1.3 %foldy_end.1 = (f32[2,4,4,30]{3,2,1,0:T(4,128)}, f32[2,4,4]{2,1,0:T(4,128)}, f32[8,2048]{1,0:T(8,128)}) custom-call(f32[8,128]{1,0:T(8,128)S(1)} %get-tuple-element.22.sums_ref, f32[8,128]{1,0:T(8,128)S(1)} %get-tuple-element.23.once_ref, bf16[256,256]{1,0:T(8,128)(2,1)S(1)} %get-tuple-element.24.full_ref, f32[8,2048]{1,0:T(8,128)S(1)} %get-tuple-element.25.field, ...), custom_call_target="tpu_custom_call" | custom-call | tf_op jit(solution)/shard_map/foldy_end/pallas_call | solution.py:498
